TPU v7x, 512 devices: a whole 4x8x8 slice. The times are simulated.
512 devices in a mesh: dp: 8 (over y_hi, core), ep: 64 (over x, y_lo, z).
Axes of the slice: x: 4, y: 8 (y_hi: 4, y_lo: 2; y = y_hi * 2 + y_lo), z: 8, core: 2. Of those that a mesh axis runs over, the one named last changes fastest.
Arguments:
- hidden_in: bfloat16 [12288, 4096], P(('dp', 'ep')), may hold values from -6 to 6
- expert_ids: int32 [12288, 2], P(('dp', 'ep')), may hold values from 0 to 63, all different within a row; in each aligned block of 24 rows (0 to 23, 24 to 47, ...) at most 2 rows name the same one
- route_logits: float32 [12288, 64], P(('dp', 'ep')), may hold values from -10 to 10
- first_weight: bfloat16 [64, 4096, 1024], P('ep', None, 'dp'), may hold values from -0.09375 to 0.09375
- second_weight: bfloat16 [64, 1024, 4096], P('ep', None, 'dp'), may hold values from -0.1875 to 0.1875
- queries: bfloat16 [12288, 2048], P(('dp', 'ep')), may hold values from -140 to 140
- span_keys: bfloat16 [12288, 2048], P(('dp', 'ep')), may hold values from -7 to 7
- span_values: bfloat16 [12288, 2048], P(('dp', 'ep')), may hold values from -6 to 6
- cache_keys: bfloat16 [512, 72, 2048], P(('dp', 'ep')), may hold values from -6 to 6
- cache_values: bfloat16 [512, 72, 2048], P(('dp', 'ep')), may hold values from -6 to 6
- valid_frames: int32 [512], P(('dp', 'ep')), may hold values from 1 to 3
Outputs:
- mixed: bfloat16 [12288, 4096], P(('dp', 'ep'))
- attended: bfloat16 [12288, 2048], P(('dp', 'ep'))
Inputs may be any that keep to these rules, and one draw needn't show every extreme that they name: `expert_ids`: each token names two different experts. In the rows of one device (24 rows) no expert is named more than 2 times, a bound that some block reaches.
All inputs are finite; a program needn't handle non-finite values.
Results may differ from a plain program's by a relative error of at most 0.0057.
Values may be sent and summed in bfloat16 or wider, within the bound.
A program may use at most 128 MiB of HBM per device.

v0:
```python
import math
import jax
import jax.numpy as jnp
from jax import lax
from jax.sharding import PartitionSpec as P

HEADS = 16
HEAD_DIM = 128
FRAME_TOK = 24


def activate(pre):
    return jax.nn.gelu(pre, approximate=True).astype(jnp.bfloat16)


def expert_slots(expert_ids):
    flat_ids = expert_ids.reshape(-1)
    assigned = flat_ids.shape[0]
    row_ids = lax.broadcasted_iota(jnp.int32, (assigned, assigned), 0)
    col_ids = lax.broadcasted_iota(jnp.int32, (assigned, assigned), 1)
    same_expert = (flat_ids[:, None] == flat_ids[None, :]) & (col_ids < row_ids)
    return jnp.sum(same_expert.astype(jnp.int32), axis=1).reshape(expert_ids.shape)


def attend(queries, span_keys, span_values, cache_keys, cache_values, valid_count):
    token_count = queries.shape[0]
    cache_len = cache_keys.shape[0]
    key_rows = jnp.concatenate([cache_keys, span_keys], axis=0)
    value_rows = jnp.concatenate([cache_values, span_values], axis=0)
    query_heads = queries.reshape(token_count, HEADS, HEAD_DIM)
    key_heads = key_rows.reshape(-1, HEADS, HEAD_DIM)
    value_heads = value_rows.reshape(-1, HEADS, HEAD_DIM)
    scores = jnp.einsum(
        "thd,khd->htk", query_heads, key_heads, preferred_element_type=jnp.float32
    ) * (1.0 / math.sqrt(HEAD_DIM))
    position = lax.broadcasted_iota(jnp.int32, (key_rows.shape[0],), 0)
    usable = (position >= cache_len) | (position // FRAME_TOK < valid_count)
    scores = jnp.where(usable[None, None, :], scores, -1e30)
    row_max = jnp.max(scores, axis=2, keepdims=True)
    weights = jnp.exp(scores - row_max)
    weights = (weights / jnp.sum(weights, axis=2, keepdims=True)).astype(jnp.bfloat16)
    result = jnp.einsum("htk,khd->thd", weights, value_heads, preferred_element_type=jnp.float32)
    return result.astype(jnp.bfloat16).reshape(token_count, HEADS * HEAD_DIM)


def shards(
    hidden_in,
    expert_ids,
    route_logits,
    first_weight,
    second_weight,
    queries,
    span_keys,
    span_values,
    cache_keys,
    cache_values,
    valid_frames,
):
    tokens, model_width = hidden_in.shape
    experts = lax.axis_size("ep")
    capacity = max(2, 8 * tokens // (3 * experts))
    slots = expert_slots(expert_ids)
    places = expert_ids * capacity + slots
    place_ids = lax.broadcasted_iota(jnp.int32, (tokens, experts * capacity), 1)
    picks = [places[:, column : column + 1] == place_ids for column in range(2)]
    chooser = (picks[0] | picks[1]).astype(jnp.bfloat16)
    dispatch = lax.dot_general(
        chooser, hidden_in, (((0,), (0,)), ((), ())), preferred_element_type=jnp.float32
    )
    dispatch = dispatch.astype(jnp.bfloat16).reshape(experts, capacity, model_width)
    expert_cols = lax.broadcasted_iota(jnp.int32, route_logits.shape, 1)
    chosen = jnp.stack(
        [
            jnp.sum(
                jnp.where(expert_cols == expert_ids[:, column : column + 1], route_logits, 0.0),
                axis=1,
            )
            for column in range(2)
        ],
        axis=1,
    )
    gates = jax.nn.softmax(chosen, axis=1)
    first_local = first_weight[0]
    second_local = second_weight[0]
    received = lax.all_to_all(dispatch, "ep", split_axis=0, concat_axis=0, tiled=True)
    sources, item_count, _ = received.shape
    expert_rows = received.reshape(sources * item_count, model_width)
    hidden = activate(
        jnp.dot(
            expert_rows,
            lax.all_gather(first_local, "dp", axis=1, tiled=True),
            preferred_element_type=jnp.float32,
        )
    )
    result = jnp.dot(
        hidden,
        lax.all_gather(second_local, "dp", axis=1, tiled=True),
        preferred_element_type=jnp.float32,
    ).astype(jnp.bfloat16)
    outputs = result.reshape(sources, item_count, model_width)
    returned = lax.all_to_all(outputs, "ep", split_axis=0, concat_axis=0, tiled=True)
    attended = attend(
        queries, span_keys, span_values, cache_keys[0], cache_values[0], valid_frames[0]
    )
    flat_back = returned.reshape(experts * capacity, model_width)
    running = jnp.zeros((tokens, model_width), jnp.float32)
    for column in range(2):
        picked = jnp.dot(
            picks[column].astype(jnp.bfloat16), flat_back, preferred_element_type=jnp.float32
        )
        running = running + gates[:, column : column + 1] * picked
    mixed = running.astype(jnp.bfloat16)
    return (mixed, attended)


def solution(mesh):
    placed = (
        P(("dp", "ep"), None),
        P(("dp", "ep"), None),
        P(("dp", "ep"), None),
        P("ep", None, "dp"),
        P("ep", None, "dp"),
        P(("dp", "ep"), None),
        P(("dp", "ep"), None),
        P(("dp", "ep"), None),
        P(("dp", "ep"), None, None),
        P(("dp", "ep"), None, None),
        P(("dp", "ep")),
    )
    return jax.shard_map(
        shards,
        mesh=mesh,
        in_specs=placed,
        out_specs=(P(("dp", "ep"), None), P(("dp", "ep"), None)),
        check_vma=False,
    )
```

profile of v0, /device:TPU:2, one launch (start us, length us, event | category | flops | bytes accessed | tf_op | source)
XLA Modules:
  0.0 263.9 jit_solution(3099905430017032602)
XLA Ops:
  7.2 0.0 copy-start
  7.2 0.0 all-gather.7.cloned.1.call-start
  7.2 0.7 all-gather.7.cloned.1.call-update
  7.9 0.0 all-gather.5.cloned.1.call-start
  8.0 0.7 all-gather.5.cloned.1.call-update
  8.7 0.8 copy.35
  9.4 0.1 eq.61
  9.5 0.2 convert_reduce_fusion
  9.7 0.1 reshape.64
  9.8 0.1 copy.36
  9.9 0.7 multiply_add_fusion
  10.6 0.0 copy-done
  10.6 0.5 convolution_convert_fusion
  11.1 0.7 reshape.65
  11.9 52.7 %all_to_all.10 = bf16[64,2,4096]{2,1,0:T(2,128)(2,1)S(1)} all-to-all(bf16[64,2,4096]{2,1,0:T(2,128)(2,1)S(1)} %reshape.65), channel_id=1, replica_groups=mesh['dp'=8,'ep'=64] {'ep'}, dimensions={0} | all-to-all | bytes 2097152 | tf_op jit(solution)/shard_map/all_to_all | solution.py:85
  64.5 0.4 reshape.66
  64.9 0.0 copy-start.1
  65.0 0.0 copy-start.2
  65.0 0.0 copy-start.3
  65.0 0.0 copy-start.4
  65.0 0.0 copy-start.7
  65.0 45.3 %all-gather.7.cloned.1.call-done = bf16[1,1024,4096]{2,1,0:T(8,128)(2,1)} async-done(((bf16[1,1024,512]{2,1,0:T(8,128)(2,1)}), bf16[1,1024,4096]{2,1,0:T(8,128)(2,1)}) %all-gather.7.cloned.1.call-update) | async-done | bytes 8388624 | tf_op jit(solution)/shard_map/all_gather | solution.py:97
  110.3 95.3 %all-gather.5.cloned.1.call-done = bf16[1,4096,1024]{2,1,0:T(8,128)(2,1)} async-done(((bf16[1,4096,128]{2,1,0:T(8,128)(2,1)}), bf16[1,4096,1024]{2,1,0:T(8,128)(2,1)}) %all-gather.5.cloned.1.call-update) | async-done | bytes 8388624 | tf_op jit(solution)/shard_map/all_gather | solution.py:91
  205.7 8.3 %fusion.5 = bf16[128,4096]{1,0:T(8,128)(2,1)S(1)} fusion(bf16[1,1024,4096]{2,1,0:T(8,128)(2,1)} %all-gather.7.cloned.1.call-done, bf16[128,4096]{1,0:T(8,128)(2,1)S(1)} %reshape.66, bf16[1,4096,1024]{2,1,0:T(8,128)(2,1)} %all-gather.5.cloned.1.call-done), kind=kOutput, calls=%fused_computation.5 | convolution fusion | flops 2149187584 | bytes 18874368 | tf_op jit(solution)/shard_map/dot_general | solution.py:95
  214.0 0.0 copy-start.6
  214.0 0.0 copy-start.5
  214.0 1.5 reshape.67
  215.5 10.9 %all-to-all-start.1 = ((bf16[64,2,4096]{2,1,0:T(2,128)(2,1)}), bf16[64,2,4096]{2,1,0:T(2,128)(2,1)S(1)}, u32[]{:S(2)}, u32[]{:S(2)}) async-start(bf16[64,2,4096]{2,1,0:T(2,128)(2,1)} %reshape.67), calls=%async_computation.1 | async-start | bytes 2097152 | tf_op jit(solution)/shard_map/all_to_all | solution.py:101
  226.4 0.0 copy-done.1
  226.5 0.1 copy.37
  226.6 0.0 copy-done.2
  226.6 0.1 copy.39
  227.4 0.0 copy-done.3
  227.4 0.0 copy-done.4
  227.5 0.0 copy-done.7
  227.5 0.5 fusion.70
  227.9 0.3 fusion.14
  228.2 0.7 copy.62
  228.9 0.0 copy-done.6
  228.9 0.0 copy-done.5
  228.9 0.2 select_reduce_fusion
  229.2 26.1 %all-to-all-done.1 = bf16[64,2,4096]{2,1,0:T(2,128)(2,1)S(1)} async-done(((bf16[64,2,4096]{2,1,0:T(2,128)(2,1)}), bf16[64,2,4096]{2,1,0:T(2,128)(2,1)S(1)}, u32[]{:S(2)}, u32[]{:S(2)}) %all-to-all-start.1) | async-done | bytes 1048608 | tf_op jit(solution)/shard_map/all_to_all | solution.py:101
  255.3 0.4 reshape.68
  255.7 0.3 convolution_multiply_fusion.1
  256.0 1.0 fusion.9
  (11 shorter events, 0.2 us)
Async XLA Ops:
  7.2 3.4 %copy-start = (bf16[24,4096]{1,0:T(8,128)(2,1)S(1)}, bf16[24,4096]{1,0:T(8,128)(2,1)}, u32[]{:S(2)}) copy-start(bf16[24,4096]{1,0:T(8,128)(2,1)} %param.11) | copy-start | bytes 589828
  7.2 103.1 %all-gather.7.cloned.1.call-start = ((), (), s32[]{:S(2)}) async-start(), calls=%async_computation.3 | async-start | bytes 9437184 | tf_op jit(solution)/shard_map/all_gather | solution.py:97
  7.9 197.7 %all-gather.5.cloned.1.call-start = ((), (), s32[]{:S(2)}) async-start(), calls=%async_computation.2 | async-start | bytes 9437184 | tf_op jit(solution)/shard_map/all_gather | solution.py:91
  64.9 161.5 %copy-start.1 = (bf16[1,72,2048]{2,1,0:T(8,128)(2,1)S(1)}, bf16[1,72,2048]{2,1,0:T(8,128)(2,1)}, u32[]{:S(2)}) copy-start(bf16[1,72,2048]{2,1,0:T(8,128)(2,1)} %param.20) | copy-start | bytes 884740
  65.0 161.6 %copy-start.2 = (bf16[1,72,2048]{2,1,0:T(8,128)(2,1)S(1)}, bf16[1,72,2048]{2,1,0:T(8,128)(2,1)}, u32[]{:S(2)}) copy-start(bf16[1,72,2048]{2,1,0:T(8,128)(2,1)} %param.19) | copy-start | bytes 884740
  65.0 162.4 %copy-start.3 = (bf16[24,2048]{1,0:T(8,128)(2,1)S(1)}, bf16[24,2048]{1,0:T(8,128)(2,1)}, u32[]{:S(2)}) copy-start(bf16[24,2048]{1,0:T(8,128)(2,1)} %param.18) | copy-start | bytes 294916
  65.0 162.4 %copy-start.4 = (bf16[24,2048]{1,0:T(8,128)(2,1)S(1)}, bf16[24,2048]{1,0:T(8,128)(2,1)}, u32[]{:S(2)}) copy-start(bf16[24,2048]{1,0:T(8,128)(2,1)} %param.17) | copy-start | bytes 294916
  65.0 162.5 %copy-start.7 = (bf16[24,2048]{1,0:T(8,128)(2,1)S(1)}, bf16[24,2048]{1,0:T(8,128)(2,1)}, u32[]{:S(2)}) copy-start(bf16[24,2048]{1,0:T(8,128)(2,1)} %param.16) | copy-start | bytes 294916
  214.0 14.9 %copy-start.6 = (s32[24,2]{0,1:T(2,128)S(1)}, s32[24,2]{0,1:T(2,128)}, u32[]{:S(2)}) copy-start(s32[24,2]{0,1:T(2,128)} %param.12) | copy-start | bytes 580
  214.0 14.9 %copy-start.5 = (f32[24,64]{1,0:T(8,128)S(1)}, f32[24,64]{1,0:T(8,128)}, u32[]{:S(2)}) copy-start(f32[24,64]{1,0:T(8,128)} %param.13) | copy-start | bytes 18436
  215.5 39.8 %all-to-all-start.1 = ((bf16[64,2,4096]{2,1,0:T(2,128)(2,1)}), bf16[64,2,4096]{2,1,0:T(2,128)(2,1)S(1)}, u32[]{:S(2)}, u32[]{:S(2)}) async-start(bf16[64,2,4096]{2,1,0:T(2,128)(2,1)} %reshape.67), calls=%async_computation.1 | async-start | bytes 2097152 | tf_op jit(solution)/shard_map/all_to_all | solution.py:101
Sparse Core Ops, SparseCore 0:
  10.1 100.1 all-gather.6
  112.4 93.1 all-gather.4
where the time goes:
time: 264 us
  waiting for transfers between devices  168 us (64%)
  blocking collectives  52.7 us (20%)
  between operations  14.9 us (6%)
  starting transfers between devices  11 us (4%)
  matrix products  10.9 us (4%)
  local copies, waits for them, and re-layouts  5.07 us (2%)
    all_gather x1, waiting for transfers between devices, shards(): lax.all_gather(first_local, 'dp', axis=1, tiled=True)  95.3 us
    all_to_all x1, blocking collectives, shards(): lax.all_to_all(dispatch, 'ep', split_axis=0, concat_axis=0, tiled=True)  52.7 us
    all_gather x1, waiting for transfers between devices, shards(): lax.all_gather(second_local, 'dp', axis=1, tiled=True)  45.3 us
    all_to_all x1, waiting for transfers between devices, shards(): lax.all_to_all(outputs, 'ep', split_axis=0, concat_axis=0, tiled=True)  26.1 us
    all_to_all x1, starting transfers between devices, shards(): lax.all_to_all(outputs, 'ep', split_axis=0, concat_axis=0, tiled=True)  10.9 us
    dot_general x1, matrix products, shards(): jnp.dot(hidden, lax.all_gather(second_local, 'dp', axis=1, tiled=True), p...  8.33 us
  transfers between devices with their start and end apart: 3, of which 3 were waited for; matrix products, arithmetic and copies ran while one was open for 2% of the time, Pallas kernels for 0%

commit v1 on v0

--- a/solution.py
+++ b/solution.py
@@ -7,6 +7,11 @@
 HEADS = 16
 HEAD_DIM = 128
 FRAME_TOK = 24
+
+
+def exchange_gather(value, name, along):
+    sent = jnp.stack([value] * lax.axis_size(name))
+    return jnp.concatenate(lax.all_to_all(sent, name, 0, 0), axis=along)
 
 
 def activate(pre):
@@ -87,9 +92,7 @@
     expert_rows = received.reshape(sources * item_count, model_width)
     hidden = activate(
         jnp.dot(
-            expert_rows,
-            lax.all_gather(first_local, "dp", axis=1, tiled=True),
-            preferred_element_type=jnp.float32,
+            expert_rows, exchange_gather(first_local, "dp", 1), preferred_element_type=jnp.float32
         )
     )
     result = jnp.dot(

time: 264 us -> 374 us (1.42)
  waiting for transfers between devices: 168 us -> 306 us
  blocking collectives: 52.7 us -> 0 us
  starting transfers between devices: 11 us -> 26.7 us
  local copies, waits for them, and re-layouts: 5.07 us -> 11.8 us
    all_to_all x0 -> x2, waiting for transfers between devices: none -> 280 us  [the longest x1 253 us: exchange_gather(): return jnp.concatenate(lax.all_to_all(sent, name, 0, 0), axis=along)]
    all_gather x1 -> x0, waiting for transfers between devices: 95.3 us -> none  [shards(): lax.all_gather(first_local, 'dp', axis=1, tiled=True)]
    all_to_all x1 -> x0, blocking collectives: 52.7 us -> none  [shards(): lax.all_to_all(dispatch, 'ep', split_axis=0, concat_axis=0, tiled=True)]
    all_gather x1, waiting for transfers between devices: 45.3 us -> 0.01 us  [shards(): lax.all_gather(second_local, 'dp', axis=1, tiled=True)]
    all_to_all x0 -> x2, starting transfers between devices: none -> 21.1 us  [the longest x1 14.9 us: shards(): lax.all_to_all(dispatch, 'ep', split_axis=0, concat_axis=0, tiled=True)]
    another operation x0 -> x2, local copies, waits for them, and re-layouts: none -> 5.83 us  [the longest x1 4.35 us: exchange_gather(): sent = jnp.stack([value] * lax.axis_size(name))]
    all_to_all x1, starting transfers between devices: 10.9 us -> 5.55 us  [shards(): lax.all_to_all(outputs, 'ep', split_axis=0, concat_axis=0, tiled=True)]
  transfers between devices with their start and end apart: 3 -> 4, of which waited for: 3 -> 3; matrix products, arithmetic and copies ran while one was open for 2% -> 1% of each run, Pallas kernels for 0% -> 0%
where the time goes in v1:
time: 374 us; the launch traced here: 373 us
  waiting for transfers between devices  306 us (82%)
  starting transfers between devices  26.7 us (7%)
  between operations  14.9 us (4%)
  matrix products  12.6 us (3%)
  local copies, waits for them, and re-layouts  11.8 us (3%)
    all_to_all x1, waiting for transfers between devices, exchange_gather(): return jnp.concatenate(lax.all_to_all(sent, name, 0, 0), axis=along)  253 us
    all_to_all x1, waiting for transfers between devices, shards(): lax.all_to_all(dispatch, 'ep', split_axis=0, concat_axis=0, tiled=True)  27 us
    all_to_all x1, waiting for transfers between devices, shards(): lax.all_to_all(outputs, 'ep', split_axis=0, concat_axis=0, tiled=True)  25.4 us
    all_to_all x1, starting transfers between devices, shards(): lax.all_to_all(dispatch, 'ep', split_axis=0, concat_axis=0, tiled=True)  14.9 us
    dot_general x1, matrix products, shards(): jnp.dot(hidden, lax.all_gather(second_local, 'dp', axis=1, tiled=True), p...  9.95 us
  transfers between devices with their start and end apart: 4, of which 3 were waited for; matrix products, arithmetic and copies ran while one was open for 1% of the time, Pallas kernels for 0%

profile of v1, /device:TPU:2, one launch (start us, length us, event | category | flops | bytes accessed | tf_op | source)
XLA Modules:
  0.0 373.2 jit_solution(10964587880860550526)
XLA Ops:
  7.2 0.0 copy-start
  7.2 0.8 copy.37
  8.0 0.1 eq.61
  8.1 0.2 convert_reduce_fusion
  8.3 0.1 reshape.71
  8.4 0.1 copy.38
  8.4 0.7 multiply_add_fusion
  9.1 0.0 copy-done
  9.1 0.5 convolution_convert_fusion
  9.7 1.5 reshape.72
  11.2 14.9 %all-to-all-start = ((bf16[64,2,4096]{2,1,0:T(2,128)(2,1)}), bf16[64,2,4096]{2,1,0:T(2,128)(2,1)S(1)}, u32[]{:S(2)}, u32[]{:S(2)}) async-start(bf16[64,2,4096]{2,1,0:T(2,128)(2,1)} %reshape.72), calls=%async_computation | async-start | bytes 2097152 | tf_op jit(solution)/shard_map/all_to_all | solution.py:90
  26.1 1.5 copy.39
  27.6 27.0 %all-to-all-done = bf16[64,2,4096]{2,1,0:T(2,128)(2,1)S(1)} async-done(((bf16[64,2,4096]{2,1,0:T(2,128)(2,1)}), bf16[64,2,4096]{2,1,0:T(2,128)(2,1)S(1)}, u32[]{:S(2)}, u32[]{:S(2)}) %all-to-all-start) | async-done | bytes 1048608 | tf_op jit(solution)/shard_map/all_to_all | solution.py:90
  54.6 4.3 %stack.15 = bf16[8,4096,128]{1,2,0:T(8,128)(2,1)} broadcast(bf16[4096,128]{0,1:T(8,128)(2,1)S(1)} %copy.39), dimensions={1,2} | broadcast | bytes 9437184 | tf_op jit(solution)/shard_map/stack | solution.py:13
  58.9 6.2 %all-to-all-start.1 = ((bf16[8,4096,128]{1,2,0:T(8,128)(2,1)}), bf16[8,4096,128]{1,2,0:T(8,128)(2,1)}, u32[]{:S(2)}, u32[]{:S(2)}) async-start(bf16[8,4096,128]{1,2,0:T(8,128)(2,1)} %stack.15), calls=%async_computation.1 | async-start | bytes 16777216 | tf_op jit(solution)/shard_map/all_to_all | solution.py:14
  65.1 0.0 all-gather.3.cloned.1.call-start
  65.2 0.7 all-gather.3.cloned.1.call-update
  65.8 0.4 reshape.73
  66.3 253.1 %all-to-all-done.1 = bf16[8,4096,128]{1,2,0:T(8,128)(2,1)} async-done(((bf16[8,4096,128]{1,2,0:T(8,128)(2,1)}), bf16[8,4096,128]{1,2,0:T(8,128)(2,1)}, u32[]{:S(2)}, u32[]{:S(2)}) %all-to-all-start.1) | async-done | bytes 8388640 | tf_op jit(solution)/shard_map/all_to_all | solution.py:14
  319.4 0.0 all-gather.3.cloned.1.call-done
  319.4 0.0 copy-start.1
  319.4 0.0 copy-start.2
  319.4 0.0 copy-start.3
  319.4 0.0 copy-start.4
  319.4 0.0 copy-start.7
  319.4 9.9 %fusion.3 = bf16[128,4096]{1,0:T(8,128)(2,1)S(1)} fusion(bf16[1,1024,4096]{2,1,0:T(8,128)(2,1)} %all-gather.3.cloned.1.call-done, bf16[128,4096]{1,0:T(8,128)(2,1)S(1)} %reshape.73, bf16[4096,1024]{0,1:T(8,128)(2,1)} %bitcast.9), kind=kOutput, calls=%fused_computation.3 | convolution fusion | flops 2149187584 | bytes 18874368 | tf_op jit(solution)/shard_map/dot_general | solution.py:98
  329.4 0.0 copy-start.6
  329.4 0.0 copy-start.5
  329.4 1.5 reshape.76
  330.9 5.6 %all-to-all-start.2 = ((bf16[64,2,4096]{2,1,0:T(2,128)(2,1)}), bf16[64,2,4096]{2,1,0:T(2,128)(2,1)S(1)}, u32[]{:S(2)}, u32[]{:S(2)}) async-start(bf16[64,2,4096]{2,1,0:T(2,128)(2,1)} %reshape.76), calls=%async_computation.2 | async-start | bytes 2097152 | tf_op jit(solution)/shard_map/all_to_all | solution.py:104
  336.5 0.0 copy-done.1
  336.5 0.1 copy.42
  337.3 0.0 copy-done.2
  337.3 0.1 copy.40
  337.4 0.0 copy-done.3
  337.5 0.0 copy-done.4
  337.5 0.0 copy-done.7
  337.5 0.5 fusion.63
  338.0 0.3 fusion.12
  338.3 0.7 copy.65
  338.9 0.0 copy-done.6
  339.0 0.0 copy-done.5
  339.0 0.2 select_reduce_fusion
  339.2 25.4 %all-to-all-done.2 = bf16[64,2,4096]{2,1,0:T(2,128)(2,1)S(1)} async-done(((bf16[64,2,4096]{2,1,0:T(2,128)(2,1)}), bf16[64,2,4096]{2,1,0:T(2,128)(2,1)S(1)}, u32[]{:S(2)}, u32[]{:S(2)}) %all-to-all-start.2) | async-done | bytes 1048608 | tf_op jit(solution)/shard_map/all_to_all | solution.py:104
  364.6 0.4 reshape.77
  365.0 0.3 convolution_multiply_fusion.1
  365.3 1.0 fusion.7
  (11 shorter events, 0.2 us)
Async XLA Ops:
  7.2 2.0 copy-start
  11.2 43.4 %all-to-all-start = ((bf16[64,2,4096]{2,1,0:T(2,128)(2,1)}), bf16[64,2,4096]{2,1,0:T(2,128)(2,1)S(1)}, u32[]{:S(2)}, u32[]{:S(2)}) async-start(bf16[64,2,4096]{2,1,0:T(2,128)(2,1)} %reshape.72), calls=%async_computation | async-start | bytes 2097152 | tf_op jit(solution)/shard_map/all_to_all | solution.py:90
  58.9 260.5 %all-to-all-start.1 = ((bf16[8,4096,128]{1,2,0:T(8,128)(2,1)}), bf16[8,4096,128]{1,2,0:T(8,128)(2,1)}, u32[]{:S(2)}, u32[]{:S(2)}) async-start(bf16[8,4096,128]{1,2,0:T(8,128)(2,1)} %stack.15), calls=%async_computation.1 | async-start | bytes 16777216 | tf_op jit(solution)/shard_map/all_to_all | solution.py:14
  65.1 254.3 %all-gather.3.cloned.1.call-start = ((), (), s32[]{:S(2)}) async-start(), calls=%async_computation.3 | async-start | bytes 9437184 | tf_op jit(solution)/shard_map/all_gather | solution.py:100
  319.4 17.1 %copy-start.1 = (bf16[1,72,2048]{2,1,0:T(8,128)(2,1)S(1)}, bf16[1,72,2048]{2,1,0:T(8,128)(2,1)}, u32[]{:S(2)}) copy-start(bf16[1,72,2048]{2,1,0:T(8,128)(2,1)} %param.19) | copy-start | bytes 884740
  319.4 17.9 %copy-start.2 = (bf16[1,72,2048]{2,1,0:T(8,128)(2,1)S(1)}, bf16[1,72,2048]{2,1,0:T(8,128)(2,1)}, u32[]{:S(2)}) copy-start(bf16[1,72,2048]{2,1,0:T(8,128)(2,1)} %param.20) | copy-start | bytes 884740
  319.4 18.0 %copy-start.3 = (bf16[24,2048]{1,0:T(8,128)(2,1)S(1)}, bf16[24,2048]{1,0:T(8,128)(2,1)}, u32[]{:S(2)}) copy-start(bf16[24,2048]{1,0:T(8,128)(2,1)} %param.17) | copy-start | bytes 294916
  319.4 18.1 %copy-start.4 = (bf16[24,2048]{1,0:T(8,128)(2,1)S(1)}, bf16[24,2048]{1,0:T(8,128)(2,1)}, u32[]{:S(2)}) copy-start(bf16[24,2048]{1,0:T(8,128)(2,1)} %param.18) | copy-start | bytes 294916
  319.4 18.1 %copy-start.7 = (bf16[24,2048]{1,0:T(8,128)(2,1)S(1)}, bf16[24,2048]{1,0:T(8,128)(2,1)}, u32[]{:S(2)}) copy-start(bf16[24,2048]{1,0:T(8,128)(2,1)} %param.16) | copy-start | bytes 294916
  329.4 9.6 %copy-start.6 = (s32[24,2]{0,1:T(2,128)S(1)}, s32[24,2]{0,1:T(2,128)}, u32[]{:S(2)}) copy-start(s32[24,2]{0,1:T(2,128)} %param.12) | copy-start | bytes 580
  329.4 9.6 %copy-start.5 = (f32[24,64]{1,0:T(8,128)S(1)}, f32[24,64]{1,0:T(8,128)}, u32[]{:S(2)}) copy-start(f32[24,64]{1,0:T(8,128)} %param.13) | copy-start | bytes 18436
  330.9 33.7 %all-to-all-start.2 = ((bf16[64,2,4096]{2,1,0:T(2,128)(2,1)}), bf16[64,2,4096]{2,1,0:T(2,128)(2,1)S(1)}, u32[]{:S(2)}, u32[]{:S(2)}) async-start(bf16[64,2,4096]{2,1,0:T(2,128)(2,1)} %reshape.76), calls=%async_computation.2 | async-start | bytes 2097152 | tf_op jit(solution)/shard_map/all_to_all | solution.py:104
Sparse Core Ops, SparseCore 0:
  68.0 189.5 all-gather.2
